TPU v7x, 32 devices: a whole 2x2x4 slice. The times are simulated.
32 devices in a mesh: owner: 4 (over z), rows: 8 (over y, x, core).
Axes of the slice: x: 2, y: 2, z: 4, core: 2. Of those that a mesh axis runs over, the one named last changes fastest.
Arguments:
- w_gate: float32 [128, 2048, 768], P('owner', 'rows'), may hold values from -0.1875 to 0.1875
- w_up: float32 [128, 2048, 768], P('owner', 'rows'), may hold values from -0.1875 to 0.1875
- router_weight: float32 [2048, 128], P('rows', 'owner'), may hold values from -0.125 to 0.125
- router_gain: float32 [2048], P('rows'), may hold values from 0.25 to 1.75
Outputs:
- serve_gate: bfloat16 [128, 2048, 768], P('owner', None, 'rows')
- serve_up: bfloat16 [128, 2048, 768], P('owner', None, 'rows')
- scale_gate: float32 [128, 768], P('owner', 'rows')
- scale_up: float32 [128, 768], P('owner', 'rows')
- serve_router: bfloat16 [2048, 128], replicated
All inputs are finite; a program needn't handle non-finite values. Where the computation divides by a largest or mean magnitude, that divisor is 1e-20 or more.
Results may differ from a plain program's by a relative error of at most 0.001.
Values may be sent and summed in bfloat16 or wider, within the bound.
A program may use at most 192 MiB of HBM per device.

v0:
```python
import functools

import jax
import jax.numpy as jnp
from jax import lax
from jax.experimental import pallas as pl
from jax.experimental.pallas import tpu as pltpu
from jax.sharding import PartitionSpec as P

MESH = pl.DeviceIdType.MESH
WINDOW = 6
LOADS = 3
PAIR_LAG = 2
CHIP_LAG = 5
LAG = 7
HELD = LOADS + LAG
SUMS = 2 * LAG + 2
GROUP = 4


def peer_steps(n):
    far = list(range(2, n, 2))
    return far + [k + 1 for k in far] + [1]


def toggled(index, k):
    result, bit = index, 1
    while bit <= k:
        if k & bit:
            result = result + bit * (1 - 2 * lax.rem(index // bit, 2))
        bit *= 2
    return result


def exchange(
    experts, n, owners, depth,
    gate, up, router, gain,
    pieces, routed, scales,
    window, stage, row_block, part, partner, both, others, whole,
    load_sem, send_sem, recv_sem, self_sem, pair_send, pair_recv, sum_send, sum_recv, last_send, last_recv,
    own_sem, z_send, z_recv, r_send, r_recv, c_send, c_recv,
):
    me, mine = lax.axis_index("rows"), lax.axis_index("owner")
    units, piece, width = 2 * experts, pieces.shape[2], gate.shape[2]
    peers = [toggled(me, k) for k in peer_steps(n)]
    alike = [toggled(me, k) for k in range(2, n, 2)]
    core, beside = lax.rem(me, 2), toggled(me, 1)
    columns = [lax.rem(mine + k, owners) for k in range(1, owners)]

    barrier = pltpu.get_barrier_semaphore()
    for p in peers:
        pl.semaphore_signal(barrier, inc=1, device_id=(mine, p), device_id_type=MESH)
    for c in columns:
        pl.semaphore_signal(barrier, inc=1, device_id=(c, me), device_id_type=MESH)

    def load(s, go):
        for matrix, first in ((gate, 0), (up, experts)):
            @pl.when((s >= first) & (s < first + experts))
            def _():
                slot = lax.rem(s, HELD)
                copy = pltpu.make_async_copy(matrix.at[s - first], window.at[slot], load_sem.at[slot])
                copy.start() if go else copy.wait()

    def pair(s):
        slot = lax.rem(s, SUMS)
        return pltpu.make_async_remote_copy(
            part.at[s, 1 - core], partner.at[s], pair_send.at[slot], pair_recv.at[slot],
            device_id=(mine, beside), device_id_type=MESH,
        )

    def halves(s):
        slot = lax.rem(s, SUMS)
        return pltpu.make_async_remote_copy(
            whole.at[s, core], whole.at[s, core], last_send.at[slot], last_recv.at[slot],
            device_id=(mine, beside), device_id_type=MESH,
        )

    def chips(s):
        slot = lax.rem(s, SUMS)
        return [
            pltpu.make_async_remote_copy(
                both.at[s], others.at[s, i], sum_send.at[slot, i], sum_recv.at[slot, i],
                device_id=(mine, p), device_id_type=MESH,
            )
            for i, p in enumerate(alike)
        ]

    def parts(s):
        slot, land = lax.rem(s, WINDOW), lax.rem(s, 2 * WINDOW)

        def cut(p):
            return stage.at[slot, pl.ds(pl.multiple_of(p * piece, piece), piece)]

        far = [
            pltpu.make_async_remote_copy(
                cut(p), pieces.at[s, me], send_sem.at[slot, i], recv_sem.at[land, i],
                device_id=(mine, p), device_id_type=MESH,
            )
            for i, p in enumerate(peers)
        ]
        return far, pltpu.make_async_copy(cut(me), pieces.at[s, me], self_sem.at[slot])

    def send(s):
        far, near = parts(s)
        for copy in far:
            copy.start()
        near.start()

    def settle(s):
        far, near = parts(s)
        for copy in far:
            copy.wait()
        near.wait()

    def summed(s):
        half = width // 2
        for h in range(2):
            w = window[lax.rem(s, HELD), :, h * half : (h + 1) * half]
            part[s, h] = jnp.sum(jnp.abs(w), axis=0, keepdims=True)

    def scaled(s):
        slot, held = lax.rem(s, WINDOW), lax.rem(s, HELD)
        scale = jnp.concatenate([whole[s, 0], whole[s, 1]], axis=1) / depth
        scales[s] = scale
        inverse = 1.0 / scale
        for at in range(0, width, 128):
            w = window[held, :, at : at + 128] * inverse[:, at : at + 128]
            stage[slot, at : at + 128, :] = w.T.astype(jnp.bfloat16)

    row_block[...] = (router[...] * gain[...]).astype(jnp.bfloat16)
    own = pltpu.make_async_copy(row_block, routed.at[me, mine], own_sem)
    along_z = [
        pltpu.make_async_remote_copy(
            row_block, routed.at[me, mine], z_send.at[i], z_recv.at[i],
            device_id=(c, me), device_id_type=MESH,
        )
        for i, c in enumerate(columns)
    ]
    along_rows = [
        pltpu.make_async_remote_copy(
            routed.at[me], routed.at[me], r_send.at[i], r_recv.at[i],
            device_id=(mine, p), device_id_type=MESH,
        )
        for i, p in enumerate(alike)
    ]
    across_chip = [
        pltpu.make_async_remote_copy(
            routed.at[p], routed.at[p], c_send.at[i], c_recv.at[i],
            device_id=(mine, beside), device_id_type=MESH,
        )
        for i, p in enumerate([me] + alike)
    ]

    for s in range(LOADS):
        load(jnp.int32(s), True)
    pl.semaphore_wait(barrier, len(peers) + len(columns))

    @pl.loop(0, units + LAG + 1)
    def _(i):
        @pl.when(i < units)
        def _():
            load(i, False)
            summed(i)

        @pl.when((i >= PAIR_LAG) & (i < units + PAIR_LAG))
        def _():
            s = i - PAIR_LAG
            pair(s).wait()
            both[s] = part[s, core] + partner[s]

        @pl.when((i >= CHIP_LAG) & (i < units + CHIP_LAG))
        def _():
            s = i - CHIP_LAG
            for copy in chips(s):
                copy.wait()
            total = both[s]
            for k in range(len(alike)):
                total = total + others[s, k]
            whole[s, core] = total

        @pl.when((i >= LAG) & (i < units + LAG))
        def _():
            s = i - LAG

            @pl.when(s >= WINDOW)
            def _():
                settle(s - WINDOW)

            halves(s).wait()
            scaled(s)

        @pl.when(i < units)
        def _():
            pair(i).start()

        @pl.when((i >= PAIR_LAG) & (i < units + PAIR_LAG))
        def _():
            for copy in chips(i - PAIR_LAG):
                copy.start()

        @pl.when((i >= CHIP_LAG) & (i < units + CHIP_LAG))
        def _():
            halves(i - CHIP_LAG).start()

        load(i + LOADS, True)

        @pl.when(i >= LAG + 1)
        def _():
            send(i - LAG - 1)

        @pl.when(i == LAG + 2)
        def _():
            own.start()
            for copy in along_z:
                copy.start()

        @pl.when(i == units // 2)
        def _():
            own.wait()
            for copy in along_z:
                copy.wait()
            for copy in along_rows:
                copy.start()

        @pl.when(i == units - units // 4)
        def _():
            for copy in along_rows:
                copy.wait()
            for copy in across_chip:
                copy.start()

    @pl.loop(max(units - WINDOW, 0), units)
    def _(s):
        settle(s)

    for copy in across_chip:
        copy.wait()


def arrange(n, routed, gate_in, up_in, gate_out, up_out, router_out):
    rest = gate_in.shape[3]
    for source, target in ((gate_in, gate_out), (up_in, up_out)):
        for p in range(n):
            target[:, :, p * rest : (p + 1) * rest] = source[:, p]

    @pl.when(pl.program_id(0) == 0)
    def _():
        for p in range(n):
            block = routed[p].astype(jnp.float32).reshape(-1, rest)
            router_out[p * rest : (p + 1) * rest, :] = block.T.astype(jnp.bfloat16)


def in_kernels(n, owners, w_gate, w_up, router_weight, router_gain):
    experts, rows, width = w_gate.shape
    piece, units, across = width // n, 2 * experts, router_weight.shape[1]
    depth = n * rows
    anywhere, vmem = pl.BlockSpec(memory_space=pl.ANY), pl.BlockSpec(memory_space=pltpu.VMEM)
    dma = pltpu.SemaphoreType.DMA
    pieces, routed, scales = pl.pallas_call(
        functools.partial(exchange, experts, n, owners, float(depth)),
        out_shape=(
            jax.ShapeDtypeStruct((units, n, piece, rows), jnp.bfloat16),
            jax.ShapeDtypeStruct((n, owners, across, rows), jnp.bfloat16),
            jax.ShapeDtypeStruct((units, 1, width), jnp.float32),
        ),
        in_specs=[anywhere, anywhere, vmem, vmem],
        out_specs=(anywhere, anywhere, vmem),
        scratch_shapes=[
            pltpu.VMEM((HELD, rows, width), jnp.float32),
            pltpu.VMEM((WINDOW, width, rows), jnp.bfloat16),
            pltpu.VMEM((across, rows), jnp.bfloat16),
            pltpu.VMEM((units, 2, 1, width // 2), jnp.float32),
            pltpu.VMEM((units, 1, width // 2), jnp.float32),
            pltpu.VMEM((units, 1, width // 2), jnp.float32),
            pltpu.VMEM((units, n // 2 - 1, 1, width // 2), jnp.float32),
            pltpu.VMEM((units, 2, 1, width // 2), jnp.float32),
            dma((HELD,)), dma((WINDOW, n - 1)), dma((2 * WINDOW, n - 1)), dma((WINDOW,)),
            dma((SUMS,)), dma((SUMS,)), dma((SUMS, n // 2 - 1)), dma((SUMS, n // 2 - 1)),
            dma((SUMS,)), dma((SUMS,)),
            dma, dma((owners,)), dma((owners,)), dma((n // 2,)), dma((n // 2,)),
            dma((n // 2,)), dma((n // 2,)),
        ],
        compiler_params=pltpu.CompilerParams(
            collective_id=0, has_side_effects=True, vmem_limit_bytes=32 * 2**20
        ),
        name="exchange",
    )(w_gate, w_up, router_weight.T, router_gain[None, :])
    own_scale = lax.dynamic_slice_in_dim(
        scales[:, 0, :], lax.axis_index("rows") * piece, piece, axis=1
    )

    group = GROUP if experts % GROUP == 0 else 1
    full = lambda shape: pl.BlockSpec(shape, lambda e: (0,) * len(shape))
    gate, up, router = pl.pallas_call(
        functools.partial(arrange, n),
        grid=(experts // group,),
        out_shape=(
            jax.ShapeDtypeStruct((experts, piece, depth), jnp.bfloat16),
            jax.ShapeDtypeStruct((experts, piece, depth), jnp.bfloat16),
            jax.ShapeDtypeStruct((depth, owners * across), jnp.bfloat16),
        ),
        in_specs=[
            full(routed.shape),
            pl.BlockSpec((group, n, piece, rows), lambda e: (e, 0, 0, 0)),
            pl.BlockSpec((group, n, piece, rows), lambda e: (experts // group + e, 0, 0, 0)),
        ],
        out_specs=(
            pl.BlockSpec((group, piece, depth), lambda e: (e, 0, 0)),
            pl.BlockSpec((group, piece, depth), lambda e: (e, 0, 0)),
            full((depth, owners * across)),
        ),
        compiler_params=pltpu.CompilerParams(
            dimension_semantics=("arbitrary",), vmem_limit_bytes=32 * 2**20
        ),
        name="arrange",
    )(routed, pieces, pieces)
    return (
        jnp.swapaxes(gate, 1, 2), jnp.swapaxes(up, 1, 2),
        own_scale[:experts], own_scale[experts:], router,
    )


def in_ops(n, w_gate, w_up, router_weight, router_gain):
    depth = n * w_gate.shape[1]
    sums = (jnp.sum(jnp.abs(w_gate), axis=1), jnp.sum(jnp.abs(w_up), axis=1))
    served, scales = [], []
    for w, total in zip((w_gate, w_up), lax.psum(sums, "rows")):
        scale = total / depth
        narrow = (w / jnp.expand_dims(scale, 1)).astype(jnp.bfloat16)
        piece = lax.all_to_all(narrow, "rows", split_axis=2, concat_axis=1, tiled=True)
        size = piece.shape[2]
        served.append(piece)
        scales.append(lax.dynamic_slice_in_dim(scale, lax.axis_index("rows") * size, size, axis=1))
    part = (router_weight * router_gain[:, None]).astype(jnp.bfloat16)
    router = lax.all_gather(part, "rows", axis=0, tiled=True)
    router = lax.all_gather(router, "owner", axis=1, tiled=True)
    return (*served, *scales, router)


def solution(mesh):
    n, owners = mesh.shape["rows"], mesh.shape["owner"]

    def on_device(w_gate, w_up, router_weight, router_gain):
        experts, rows, width = w_gate.shape
        whole_tiles = (
            rows % 128 == 0 and width % (16 * n) == 0 and width % 256 == 0
            and n & (n - 1) == 0 and n > 2 and owners > 1
        )
        if whole_tiles:
            return in_kernels(n, owners, w_gate, w_up, router_weight, router_gain)
        return in_ops(n, w_gate, w_up, router_weight, router_gain)

    placed = (P("owner", "rows", None), P("owner", "rows", None), P("rows", "owner"), P("rows"))
    return jax.shard_map(
        on_device,
        mesh=mesh,
        in_specs=placed,
        out_specs=(
            P("owner", None, "rows"),
            P("owner", None, "rows"),
            P("owner", "rows"),
            P("owner", "rows"),
            P(),
        ),
        check_vma=False,
    )
```

profile of v0, /device:TPU:1, one launch (start us, length us, event | category | flops | bytes accessed | tf_op | source)
XLA Modules:
  0.0 317.8 jit_solution(12159172679883969337)
XLA Ops:
  0.6 0.0 copy-start
  0.6 0.7 copy-done
  1.4 0.0 copy-start.1
  1.4 0.7 copy-done.1
  2.1 295.7 %exchange.1 = (bf16[64,8,96,256]{3,2,1,0:T(8,128)(2,1)}, bf16[8,4,32,256]{3,2,1,0:T(8,128)(2,1)S(1)}, f32[64,1,768]{2,1,0:T(1,128)S(1)}) custom-call(f32[32,256,768]{2,1,0:T(8,128)} %gate.1, f32[32,256,768]{2,1,0:T(8,128)} %up.1, f32[32,256]{1,0:T(8,128)S(1)} %bitcast.6, f32[1,256]{1,0:T(1,128)S(1)} %bitcast.7), custom_call_target="tpu_custom_call" | custom-call | tf_op jit(solution)/shard_map/exchange/pallas_call | solution.py:259
  297.8 0.8 constant_dynamic-slice_fusion.1
  298.6 19.2 %arrange.1 = (bf16[32,96,2048]{2,1,0:T(8,128)(2,1)}, bf16[32,96,2048]{2,1,0:T(8,128)(2,1)}, bf16[2048,128]{1,0:T(8,128)(2,1)}) custom-call(bf16[8,4,32,256]{3,2,1,0:T(8,128)(2,1)S(1)} %get-tuple-element.11.routed, bf16[64,8,96,256]{3,2,1,0:T(8,128)(2,1)} %get-tuple-element.12.gate_in.up_in, bf16[64,8,96,256]{3,2,1,0:T(8,128)(2,1)} %get-tuple-element.12.gate_in.up_in), custom_call_target="tpu_custom_call" | custom-call | tf_op jit(solution)/shard_map/arrange/pallas_call | solution.py:294
Async XLA Ops:
  0.6 0.8 copy-start
  1.4 0.7 copy-start.1
where the time goes:
time: 318 us
  Pallas kernels  315 us (99%)
    pallas_call x1, Pallas kernels, in_kernels(): pl.pallas_call(functools.partial(exchange, experts, n, owners, float(dept...  296 us
    pallas_call x1, Pallas kernels, in_kernels(): pl.pallas_call(functools.partial(arrange, n), grid=(experts // group,), o...  19.2 us

commit v1 on v0

v1 whole, which is shorter than its diff:
```python
import functools

import jax
import jax.numpy as jnp
from jax import lax
from jax.experimental import pallas as pl
from jax.experimental.pallas import tpu as pltpu
from jax.sharding import PartitionSpec as P

MESH = pl.DeviceIdType.MESH
WINDOW = 3
LOADS = 3
LEAD = 8
X_LAG, Y_LAG, HALF_LAG = 1, 4, 7
HELD = LOADS + LEAD
SUMS = 2 * LEAD + 2
WRITES = 4


def peer_steps(n):
    far = list(range(2, n, 2))
    return far + [k + 1 for k in far] + [1]


def toggled(index, k):
    result, bit = index, 1
    while bit <= k:
        if k & bit:
            result = result + bit * (1 - 2 * lax.rem(index // bit, 2))
        bit *= 2
    return result


def exchange(
    experts, n, owners, depth, steps,
    gate, up, router, gain,
    pieces, routed, scales,
    window, stage, weight, gains, part, early, partner, chip, others, whole,
    load_sem, send_sem, recv_sem, pair_send, pair_recv, sum_send, sum_recv, last_send, last_recv,
    early_send, early_recv, in_sem, r_send, r_recv, z_send, z_recv, c_send, c_recv,
):
    me, mine = lax.axis_index("rows"), lax.axis_index("owner")
    units, piece, rows, width = 2 * experts, pieces.shape[1], gate.shape[1], gate.shape[2]
    lead = early.shape[1]
    peers = [toggled(me, k) for k in peer_steps(n)]
    alike = [toggled(me, k) for k in range(2, n, 2)]
    core, beside = lax.rem(me, 2), toggled(me, 1)
    columns = [lax.rem(mine + k, owners) for k in range(1, owners)]

    barrier = pltpu.get_barrier_semaphore()
    for p in peers:
        pl.semaphore_signal(barrier, inc=1, device_id=(mine, p), device_id_type=MESH)
    for c in columns:
        pl.semaphore_signal(barrier, inc=1, device_id=(c, me), device_id_type=MESH)

    def load(s, go):
        for matrix, first in ((gate, 0), (up, experts)):
            @pl.when((s >= first) & (s < first + experts))
            def _():
                slot = lax.rem(s, HELD)
                copy = pltpu.make_async_copy(matrix.at[s - first], window.at[slot], load_sem.at[slot])
                copy.start() if go else copy.wait()

    def pair(s):
        slot = lax.rem(s, SUMS)
        return pltpu.make_async_remote_copy(
            part.at[s, 1 - core], partner.at[s], pair_send.at[slot], pair_recv.at[slot],
            device_id=(mine, beside), device_id_type=MESH,
        )

    def chips(s, t):
        slot = lax.rem(s, SUMS)
        return pltpu.make_async_remote_copy(
            chip.at[s, t], others.at[s, t], sum_send.at[slot, t], sum_recv.at[slot, t],
            device_id=(mine, toggled(me, steps[t])), device_id_type=MESH,
        )

    def halves(s):
        slot = lax.rem(s, SUMS)
        return pltpu.make_async_remote_copy(
            whole.at[s, core], whole.at[s, core], last_send.at[slot], last_recv.at[slot],
            device_id=(mine, beside), device_id_type=MESH,
        )

    def direct(g):
        first, count = ((0, 1), (1, lead - 1))[g]
        return [
            pltpu.make_async_remote_copy(
                part.at[pl.ds(first, count)], early.at[me, pl.ds(first, count)],
                early_send.at[g, i], early_recv.at[g, i],
                device_id=(mine, p), device_id_type=MESH,
            )
            for i, p in enumerate(peers)
        ]

    def far(s):
        slot, land = lax.rem(s, WINDOW), lax.rem(s, 2 * WINDOW)
        return [
            pltpu.make_async_remote_copy(
                stage.at[slot, pl.ds(pl.multiple_of(p * piece, piece), piece)],
                pieces.at[s, :, pl.ds(pl.multiple_of(me * rows, rows), rows)],
                send_sem.at[slot, i], recv_sem.at[land, i],
                device_id=(mine, p), device_id_type=MESH,
            )
            for i, p in enumerate(peers)
        ]

    def start(copies):
        for copy in copies:
            copy.start()

    def finish(copies):
        for copy in copies:
            copy.wait()

    def summed(s):
        half = width // 2
        for h in range(2):
            w = window[lax.rem(s, HELD), :, h * half : (h + 1) * half]
            part[s, h] = jnp.sum(jnp.abs(w), axis=0, keepdims=True)

    def early_total(first, last):
        for h in range(2):
            total = jnp.zeros((last - first, 1, width // 2), jnp.float32)
            for p in range(n):
                total = total + jnp.where(p == me, part[first:last, h], early[p, first:last, h])
            whole[first:last, h] = total

    def scaled(s):
        slot, held = lax.rem(s, WINDOW), lax.rem(s, HELD)
        scale = jnp.concatenate([whole[s, 0], whole[s, 1]], axis=1) / depth
        scales[s] = scale
        inverse = 1.0 / scale
        for at in range(0, width, 128):
            w = window[held, :, at : at + 128] * inverse[:, at : at + 128]
            stage[slot, at : at + 128, :] = w.T.astype(jnp.bfloat16)
        own = stage[slot, pl.ds(pl.multiple_of(me * piece, piece), piece), :]
        pieces[s, :, pl.ds(pl.multiple_of(me * rows, rows), rows)] = own

    fetch = [
        pltpu.make_async_copy(router, weight, in_sem.at[0]),
        pltpu.make_async_copy(gain, gains, in_sem.at[1]),
    ]
    along_rows = [
        pltpu.make_async_remote_copy(
            routed.at[me, mine], routed.at[me, mine], r_send.at[i], r_recv.at[i],
            device_id=(mine, p), device_id_type=MESH,
        )
        for i, p in enumerate(alike)
    ]
    along_z = [
        pltpu.make_async_remote_copy(
            routed.at[p, mine], routed.at[p, mine], z_send.at[i, j], z_recv.at[i, j],
            device_id=(c, me), device_id_type=MESH,
        )
        for i, p in enumerate([me] + alike)
        for j, c in enumerate(columns)
    ]
    across_chip = [
        pltpu.make_async_remote_copy(
            routed.at[p], routed.at[p], c_send.at[i], c_recv.at[i],
            device_id=(mine, beside), device_id_type=MESH,
        )
        for i, p in enumerate([me] + alike)
    ]

    for s in range(LOADS):
        load(jnp.int32(s), True)
    load(jnp.int32(0), False)
    summed(jnp.int32(0))
    load(jnp.int32(LOADS), True)
    pl.semaphore_wait(barrier, len(peers) + len(columns))
    start(direct(0))

    @pl.loop(1, lead)
    def _(s):
        load(s, False)
        summed(s)
        load(s + LOADS, True)

    start(direct(1))
    start(fetch)

    @pl.loop(0, units)
    def _(i):
        def within(s):
            return (s >= lead) & (s < units)

        @pl.when(i >= WINDOW)
        def _():
            finish(far(i - WINDOW))

        @pl.when(i == 0)
        def _():
            finish(direct(0))
            early_total(0, 1)

        @pl.when(i == 1)
        def _():
            finish(direct(1))
            early_total(1, lead)

        @pl.when(i >= lead)
        def _():
            halves(i).wait()

        scaled(i)
        ahead = i + lead

        @pl.when(ahead < units)
        def _():
            load(ahead, False)
            summed(ahead)

        @pl.when(within(ahead - X_LAG))
        def _():
            s = ahead - X_LAG
            pair(s).wait()
            chip[s, 0] = part[s, core] + partner[s]

        @pl.when(within(ahead - Y_LAG))
        def _():
            s = ahead - Y_LAG
            chips(s, 0).wait()
            chip[s, 1] = chip[s, 0] + others[s, 0]

        @pl.when(within(ahead - HALF_LAG))
        def _():
            s = ahead - HALF_LAG
            chips(s, 1).wait()
            whole[s, core] = chip[s, 1] + others[s, 1]

        @pl.when(i == 2)
        def _():
            finish(fetch)
            routed[me, mine] = (weight[...] * gains[...]).astype(jnp.bfloat16)

        @pl.when(ahead < units)
        def _():
            pair(ahead).start()

        @pl.when(within(ahead - X_LAG))
        def _():
            chips(ahead - X_LAG, 0).start()

        @pl.when(within(ahead - Y_LAG))
        def _():
            chips(ahead - Y_LAG, 1).start()

        @pl.when(within(ahead - HALF_LAG))
        def _():
            halves(ahead - HALF_LAG).start()

        start(far(i))
        load(ahead + LOADS, True)

        @pl.when(i == 3)
        def _():
            start(along_rows)

        @pl.when(i == units // 4)
        def _():
            finish(along_rows)
            start(along_z)

        @pl.when(i == units // 2)
        def _():
            finish(along_z)
            start(across_chip)

        @pl.when(i == units - units // 4)
        def _():
            finish(across_chip)

    @pl.loop(max(units - WINDOW, 0), units)
    def _(s):
        finish(far(s))


def write_out(
    n, pieces, routed, scales, gate_out, up_out, gate_scale, up_scale, router_out,
    own, table, sems, small,
):
    experts, piece, rest = gate_out.shape[0], gate_out.shape[1], routed.shape[3]
    group = experts // WRITES
    big = [
        pltpu.make_async_copy(
            pieces.at[pl.ds(first + g * group, group)], target.at[pl.ds(g * group, group)],
            sems.at[first // experts, g],
        )
        for target, first in ((gate_out, 0), (up_out, experts))
        for g in range(WRITES)
    ]
    for copy in big:
        copy.start()
    me = lax.axis_index("rows")
    for p in range(n):
        block = routed[p].astype(jnp.float32).reshape(-1, rest)
        table[p * rest : (p + 1) * rest, :] = block.T.astype(jnp.bfloat16)

        @pl.when(me == p)
        def _():
            own[...] = scales[:, 0, p * piece : (p + 1) * piece]

    little = [
        pltpu.make_async_copy(table, router_out, small.at[0]),
        pltpu.make_async_copy(own.at[pl.ds(0, experts)], gate_scale, small.at[1]),
        pltpu.make_async_copy(own.at[pl.ds(experts, experts)], up_scale, small.at[2]),
    ]
    for copy in little:
        copy.start()
    for copy in little + big:
        copy.wait()


def in_kernels(n, owners, w_gate, w_up, router_weight, router_gain):
    experts, rows, width = w_gate.shape
    piece, units, across = width // n, 2 * experts, router_weight.shape[1]
    depth = n * rows
    steps = [1 << b for b in range(1, n.bit_length() - 1)]
    half = width // 2
    anywhere, vmem = pl.BlockSpec(memory_space=pl.ANY), pl.BlockSpec(memory_space=pltpu.VMEM)
    hbm, dma = pl.BlockSpec(memory_space=pltpu.HBM), pltpu.SemaphoreType.DMA
    pieces, routed, scales = pl.pallas_call(
        functools.partial(exchange, experts, n, owners, float(depth), steps),
        out_shape=(
            pltpu.VMEM((units, piece, depth), jnp.bfloat16),
            pltpu.VMEM((n, owners, across, rows), jnp.bfloat16),
            pltpu.VMEM((units, 1, width), jnp.float32),
        ),
        in_specs=[anywhere, anywhere, hbm, hbm],
        out_specs=(vmem, vmem, vmem),
        scratch_shapes=[
            pltpu.VMEM((HELD, rows, width), jnp.float32),
            pltpu.VMEM((WINDOW, width, rows), jnp.bfloat16),
            pltpu.VMEM((across, rows), jnp.float32),
            pltpu.VMEM((1, rows), jnp.float32),
            pltpu.VMEM((units, 2, 1, half), jnp.float32),
            pltpu.VMEM((n, LEAD, 2, 1, half), jnp.float32),
            pltpu.VMEM((units, 1, half), jnp.float32),
            pltpu.VMEM((units, 2, 1, half), jnp.float32),
            pltpu.VMEM((units, 2, 1, half), jnp.float32),
            pltpu.VMEM((units, 2, 1, half), jnp.float32),
            dma((HELD,)), dma((WINDOW, n - 1)), dma((2 * WINDOW, n - 1)),
            dma((SUMS,)), dma((SUMS,)), dma((SUMS, 2)), dma((SUMS, 2)), dma((SUMS,)), dma((SUMS,)),
            dma((2, n - 1)), dma((2, n - 1)), dma((2,)),
            dma((n // 2,)), dma((n // 2,)), dma((n // 2, owners)), dma((n // 2, owners)),
            dma((n // 2,)), dma((n // 2,)),
        ],
        compiler_params=pltpu.CompilerParams(
            collective_id=0, has_side_effects=True, vmem_limit_bytes=12 * 2**20
        ),
        name="exchange",
    )(w_gate, w_up, *(pltpu.with_memory_space_constraint(x, pltpu.HBM) for x in (router_weight.T, router_gain[None, :])))

    gate, up, gate_scale, up_scale, router = pl.pallas_call(
        functools.partial(write_out, n),
        out_shape=(
            jax.ShapeDtypeStruct((experts, piece, depth), jnp.bfloat16),
            jax.ShapeDtypeStruct((experts, piece, depth), jnp.bfloat16),
            jax.ShapeDtypeStruct((experts, piece), jnp.float32),
            jax.ShapeDtypeStruct((experts, piece), jnp.float32),
            jax.ShapeDtypeStruct((depth, owners * across), jnp.bfloat16),
        ),
        in_specs=[vmem, vmem, vmem],
        out_specs=(anywhere,) * 5,
        scratch_shapes=[
            pltpu.VMEM((units, piece), jnp.float32),
            pltpu.VMEM((depth, owners * across), jnp.bfloat16),
            dma((2, WRITES)), dma((3,)),
        ],
        compiler_params=pltpu.CompilerParams(vmem_limit_bytes=1 * 2**20),
        name="write_out",
    )(*(pltpu.with_memory_space_constraint(x, pltpu.VMEM) for x in (pieces, routed, scales)))
    return jnp.swapaxes(gate, 1, 2), jnp.swapaxes(up, 1, 2), gate_scale, up_scale, router


def in_ops(n, w_gate, w_up, router_weight, router_gain):
    depth = n * w_gate.shape[1]
    sums = (jnp.sum(jnp.abs(w_gate), axis=1), jnp.sum(jnp.abs(w_up), axis=1))
    served, scales = [], []
    for w, total in zip((w_gate, w_up), lax.psum(sums, "rows")):
        scale = total / depth
        narrow = (w / jnp.expand_dims(scale, 1)).astype(jnp.bfloat16)
        piece = lax.all_to_all(narrow, "rows", split_axis=2, concat_axis=1, tiled=True)
        size = piece.shape[2]
        served.append(piece)
        scales.append(lax.dynamic_slice_in_dim(scale, lax.axis_index("rows") * size, size, axis=1))
    part = (router_weight * router_gain[:, None]).astype(jnp.bfloat16)
    router = lax.all_gather(part, "rows", axis=0, tiled=True)
    router = lax.all_gather(router, "owner", axis=1, tiled=True)
    return (*served, *scales, router)


def solution(mesh):
    n, owners = mesh.shape["rows"], mesh.shape["owner"]

    def on_device(w_gate, w_up, router_weight, router_gain):
        experts, rows, width = w_gate.shape
        whole_tiles = (
            rows % 128 == 0 and width % (16 * n) == 0 and width % 256 == 0
            and n == 8 and owners > 1 and experts % WRITES == 0 and 2 * experts >= 2 * LEAD
        )
        if whole_tiles:
            return in_kernels(n, owners, w_gate, w_up, router_weight, router_gain)
        return in_ops(n, w_gate, w_up, router_weight, router_gain)

    placed = (P("owner", "rows", None), P("owner", "rows", None), P("rows", "owner"), P("rows"))
    return jax.shard_map(
        on_device,
        mesh=mesh,
        in_specs=placed,
        out_specs=(
            P("owner", None, "rows"),
            P("owner", None, "rows"),
            P("owner", "rows"),
            P("owner", "rows"),
            P(),
        ),
        check_vma=False,
    )
```

time: 318 us -> 296 us (0.931)
  Pallas kernels: 315 us -> 296 us
    pallas_call x1, Pallas kernels: 19.2 us -> 8.66 us  [in_kernels(): pl.pallas_call(functools.partial(write_out, n), out_shape=(jax.ShapeDtype...]
    pallas_call x1, Pallas kernels: 296 us -> 287 us  [in_kernels(): pl.pallas_call(functools.partial(exchange, experts, n, owners, float(dept...]
where the time goes in v1:
time: 296 us
  Pallas kernels  296 us (100%)
    pallas_call x1, Pallas kernels, in_kernels(): pl.pallas_call(functools.partial(exchange, experts, n, owners, float(dept...  287 us
    pallas_call x1, Pallas kernels, in_kernels(): pl.pallas_call(functools.partial(write_out, n), out_shape=(jax.ShapeDtype...  8.66 us

profile of v1, /device:TPU:1, one launch (start us, length us, event | category | flops | bytes accessed | tf_op | source)
XLA Modules:
  0.0 296.2 jit_solution(5302415735603173620)
XLA Ops:
  0.6 286.9 %exchange.1 = (bf16[64,96,2048]{2,1,0:T(8,128)(2,1)S(1)}, bf16[8,4,32,256]{3,2,1,0:T(8,128)(2,1)S(1)}, f32[64,1,768]{2,1,0:T(1,128)S(1)}) custom-call(f32[32,256,768]{2,1,0:T(8,128)} %gate.1, f32[32,256,768]{2,1,0:T(8,128)} %up.1, f32[32,256]{1,0:T(8,128)} %bitcast.4, f32[1,256]{1,0:T(1,128)} %bitcast.5), custom_call_target="tpu_custom_call" | custom-call | tf_op jit(solution)/shard_map/exchange/pallas_call | solution.py:324
  287.5 8.7 %write_out.1 = (bf16[32,96,2048]{2,1,0:T(8,128)(2,1)}, bf16[32,96,2048]{2,1,0:T(8,128)(2,1)}, f32[32,96]{1,0:T(8,128)}, f32[32,96]{1,0:T(8,128)}, bf16[2048,128]{1,0:T(8,128)(2,1)}) custom-call(bf16[64,96,2048]{2,1,0:T(8,128)(2,1)S(1)} %get-tuple-element.13.pieces, bf16[8,4,32,256]{3,2,1,0:T(8,128)(2,1)S(1)} %get-tuple-element.14.routed, ...), custom_call_target="tpu_custom_call" | custom-call | tf_op jit(solution)/shard_map/write_out/pallas_call | solution.py:356

commit v2 on v1

--- a/solution.py
+++ b/solution.py
@@ -10,8 +10,8 @@
 MESH = pl.DeviceIdType.MESH
 WINDOW = 3
 LOADS = 3
-LEAD = 8
-X_LAG, Y_LAG, HALF_LAG = 1, 4, 7
+LEAD = 6
+X_LAG, Y_LAG, HALF_LAG = 1, 3, 5
 HELD = LOADS + LEAD
 SUMS = 2 * LEAD + 2
 WRITES = 4
@@ -45,13 +45,15 @@
     peers = [toggled(me, k) for k in peer_steps(n)]
     alike = [toggled(me, k) for k in range(2, n, 2)]
     core, beside = lax.rem(me, 2), toggled(me, 1)
-    columns = [lax.rem(mine + k, owners) for k in range(1, owners)]
+    below, above = lax.max(mine - 1, 0), lax.min(mine + 1, owners - 1)
 
     barrier = pltpu.get_barrier_semaphore()
     for p in peers:
         pl.semaphore_signal(barrier, inc=1, device_id=(mine, p), device_id_type=MESH)
-    for c in columns:
-        pl.semaphore_signal(barrier, inc=1, device_id=(c, me), device_id_type=MESH)
+
+    @pl.when(mine < owners - 1)
+    def _():
+        pl.semaphore_signal(barrier, inc=1, device_id=(above, me), device_id_type=MESH)
 
     def load(s, go):
         for matrix, first in ((gate, 0), (up, experts)):
@@ -148,28 +150,72 @@
         )
         for i, p in enumerate(alike)
     ]
-    along_z = [
-        pltpu.make_async_remote_copy(
-            routed.at[p, mine], routed.at[p, mine], z_send.at[i, j], z_recv.at[i, j],
-            device_id=(c, me), device_id_type=MESH,
-        )
-        for i, p in enumerate([me] + alike)
-        for j, c in enumerate(columns)
-    ]
+    mates = [me] + alike
+
+    def relay(up, step):
+        block, side = (mine - step, 1) if up else (mine + step, 0)
+        block = lax.max(lax.min(block, owners - 1), 0)
+        return [
+            pltpu.make_async_remote_copy(
+                routed.at[p, block], routed.at[p, block],
+                z_send.at[side, step, i], z_recv.at[side, step, i],
+                device_id=(above if up else below, me), device_id_type=MESH,
+            )
+            for i, p in enumerate(mates)
+        ]
+
+    def arrival(up, step):
+        block, side = (mine - 1 - step, 1) if up else (mine + 1 + step, 0)
+        block = lax.max(lax.min(block, owners - 1), 0)
+        return [
+            pltpu.make_async_remote_copy(
+                routed.at[p, block], routed.at[p, block],
+                z_send.at[side, step, i], z_recv.at[side, step, i],
+                device_id=(above if up else below, me), device_id_type=MESH,
+            )
+            for i, p in enumerate(mates)
+        ]
+
+    def relays(turn):
+        for up, step in ((False, turn - 1), (True, turn - 2)):
+            if 0 <= step < owners - 1:
+                came = (mine > step) if up else (mine + step < owners - 1)
+                went = (mine < owners - 1) & (mine >= step) if up else (mine > 0) & (mine + step <= owners - 1)
+
+                @pl.when(came)
+                def _():
+                    for copy in arrival(up, step):
+                        copy.wait_recv()
+
+                @pl.when(went)
+                def _():
+                    for copy in relay(up, step):
+                        copy.wait_send()
+        for up, step in ((False, turn), (True, turn - 1)):
+            if 0 <= step < owners - 1:
+                went = (mine < owners - 1) & (mine >= step) if up else (mine > 0) & (mine + step <= owners - 1)
+
+                @pl.when(went)
+                def _():
+                    start(relay(up, step))
+
     across_chip = [
         pltpu.make_async_remote_copy(
             routed.at[p], routed.at[p], c_send.at[i], c_recv.at[i],
             device_id=(mine, beside), device_id_type=MESH,
         )
-        for i, p in enumerate([me] + alike)
+        for i, p in enumerate(mates)
     ]
 
+    start(fetch)
     for s in range(LOADS):
         load(jnp.int32(s), True)
     load(jnp.int32(0), False)
     summed(jnp.int32(0))
     load(jnp.int32(LOADS), True)
-    pl.semaphore_wait(barrier, len(peers) + len(columns))
+    finish(fetch)
+    routed[me, mine] = (weight[...] * gains[...]).astype(jnp.bfloat16)
+    pl.semaphore_wait(barrier, len(peers) + jnp.where(mine > 0, 1, 0))
     start(direct(0))
 
     @pl.loop(1, lead)
@@ -179,7 +225,7 @@
         load(s + LOADS, True)
 
     start(direct(1))
-    start(fetch)
+    start(along_rows)
 
     @pl.loop(0, units)
     def _(i):
@@ -230,11 +276,6 @@
             chips(s, 1).wait()
             whole[s, core] = chip[s, 1] + others[s, 1]
 
-        @pl.when(i == 2)
-        def _():
-            finish(fetch)
-            routed[me, mine] = (weight[...] * gains[...]).astype(jnp.bfloat16)
-
         @pl.when(ahead < units)
         def _():
             pair(ahead).start()
@@ -254,18 +295,17 @@
         start(far(i))
         load(ahead + LOADS, True)
 
-        @pl.when(i == 3)
-        def _():
-            start(along_rows)
-
-        @pl.when(i == units // 4)
+        @pl.when(i == LEAD)
         def _():
             finish(along_rows)
-            start(along_z)
+
+        for turn in range(owners + 1):
+            @pl.when(i == LEAD + 1 + 2 * turn)
+            def _():
+                relays(turn)
 
         @pl.when(i == units // 2)
         def _():
-            finish(along_z)
             start(across_chip)
 
         @pl.when(i == units - units // 4)
@@ -344,7 +384,7 @@
             dma((HELD,)), dma((WINDOW, n - 1)), dma((2 * WINDOW, n - 1)),
             dma((SUMS,)), dma((SUMS,)), dma((SUMS, 2)), dma((SUMS, 2)), dma((SUMS,)), dma((SUMS,)),
             dma((2, n - 1)), dma((2, n - 1)), dma((2,)),
-            dma((n // 2,)), dma((n // 2,)), dma((n // 2, owners)), dma((n // 2, owners)),
+            dma((n // 2,)), dma((n // 2,)), dma((2, owners, n // 2)), dma((2, owners, n // 2)),
             dma((n // 2,)), dma((n // 2,)),
         ],
         compiler_params=pltpu.CompilerParams(
@@ -399,7 +439,7 @@
         experts, rows, width = w_gate.shape
         whole_tiles = (
             rows % 128 == 0 and width % (16 * n) == 0 and width % 256 == 0
-            and n == 8 and owners > 1 and experts % WRITES == 0 and 2 * experts >= 2 * LEAD
+            and n == 8 and owners > 1 and experts % WRITES == 0 and experts >= LEAD + 3 + 2 * owners
         )
         if whole_tiles:
             return in_kernels(n, owners, w_gate, w_up, router_weight, router_gain)

time: 296 us -> 293 us (0.990)
  Pallas kernels: 296 us -> 292 us
    pallas_call x1, Pallas kernels: 287 us -> 283 us  [in_kernels(): pl.pallas_call(functools.partial(exchange, experts, n, owners, float(dept...]
where the time goes in v2:
time: 293 us
  Pallas kernels  292 us (100%)
    pallas_call x1, Pallas kernels, in_kernels(): pl.pallas_call(functools.partial(exchange, experts, n, owners, float(dept...  283 us
    pallas_call x1, Pallas kernels, in_kernels(): pl.pallas_call(functools.partial(write_out, n), out_shape=(jax.ShapeDtype...  8.66 us

profile of v2, /device:TPU:1, one launch (start us, length us, event | category | flops | bytes accessed | tf_op | source)
XLA Modules:
  0.0 292.6 jit_solution(15659398712857933035)
XLA Ops:
  0.6 283.3 %exchange.1 = (bf16[64,96,2048]{2,1,0:T(8,128)(2,1)S(1)}, bf16[8,4,32,256]{3,2,1,0:T(8,128)(2,1)S(1)}, f32[64,1,768]{2,1,0:T(1,128)S(1)}) custom-call(f32[32,256,768]{2,1,0:T(8,128)} %gate.1, f32[32,256,768]{2,1,0:T(8,128)} %up.1, f32[32,256]{1,0:T(8,128)} %bitcast.4, f32[1,256]{1,0:T(1,128)} %bitcast.5), custom_call_target="tpu_custom_call" | custom-call | tf_op jit(solution)/shard_map/exchange/pallas_call | solution.py:364
  283.9 8.7 %write_out.1 = (bf16[32,96,2048]{2,1,0:T(8,128)(2,1)}, bf16[32,96,2048]{2,1,0:T(8,128)(2,1)}, f32[32,96]{1,0:T(8,128)}, f32[32,96]{1,0:T(8,128)}, bf16[2048,128]{1,0:T(8,128)(2,1)}) custom-call(bf16[64,96,2048]{2,1,0:T(8,128)(2,1)S(1)} %get-tuple-element.13.pieces, bf16[8,4,32,256]{3,2,1,0:T(8,128)(2,1)S(1)} %get-tuple-element.14.routed, ...), custom_call_target="tpu_custom_call" | custom-call | tf_op jit(solution)/shard_map/write_out/pallas_call | solution.py:396

commit v3 on v2

--- a/solution.py
+++ b/solution.py
@@ -8,10 +8,10 @@
 from jax.sharding import PartitionSpec as P
 
 MESH = pl.DeviceIdType.MESH
-WINDOW = 3
+WINDOW = 2
 LOADS = 3
-LEAD = 6
-X_LAG, Y_LAG, HALF_LAG = 1, 3, 5
+LEAD = 4
+X_LAG, Y_LAG, HALF_LAG = 1, 2, 3
 HELD = LOADS + LEAD
 SUMS = 2 * LEAD + 2
 WRITES = 4
@@ -207,22 +207,24 @@
         for i, p in enumerate(mates)
     ]
 
+    load(jnp.int32(0), True)
     start(fetch)
-    for s in range(LOADS):
-        load(jnp.int32(s), True)
     load(jnp.int32(0), False)
     summed(jnp.int32(0))
-    load(jnp.int32(LOADS), True)
+    pl.semaphore_wait(barrier, len(peers) + jnp.where(mine > 0, 1, 0))
+    start(direct(0)[::-1])
+
+    @pl.loop(1, HELD)
+    def _(s):
+        load(s, True)
+
     finish(fetch)
     routed[me, mine] = (weight[...] * gains[...]).astype(jnp.bfloat16)
-    pl.semaphore_wait(barrier, len(peers) + jnp.where(mine > 0, 1, 0))
-    start(direct(0))
 
     @pl.loop(1, lead)
     def _(s):
         load(s, False)
         summed(s)
-        load(s + LOADS, True)
 
     start(direct(1))
     start(along_rows)

time: 293 us -> 292 us (level)
  no operation moved by 1% of the time
where the time goes in v3:
time: 292 us
  Pallas kernels  291 us (100%)
    pallas_call x1, Pallas kernels, in_kernels(): pl.pallas_call(functools.partial(exchange, experts, n, owners, float(dept...  283 us
    pallas_call x1, Pallas kernels, in_kernels(): pl.pallas_call(functools.partial(write_out, n), out_shape=(jax.ShapeDtype...  8.66 us

profile of v3, /device:TPU:1, one launch (start us, length us, event | category | flops | bytes accessed | tf_op | source)
XLA Modules:
  0.0 291.9 jit_solution(12421951672437361506)
XLA Ops:
  0.6 282.6 %exchange.1 = (bf16[64,96,2048]{2,1,0:T(8,128)(2,1)S(1)}, bf16[8,4,32,256]{3,2,1,0:T(8,128)(2,1)S(1)}, f32[64,1,768]{2,1,0:T(1,128)S(1)}) custom-call(f32[32,256,768]{2,1,0:T(8,128)} %gate.1, f32[32,256,768]{2,1,0:T(8,128)} %up.1, f32[32,256]{1,0:T(8,128)} %bitcast.4, f32[1,256]{1,0:T(1,128)} %bitcast.5), custom_call_target="tpu_custom_call" | custom-call | tf_op jit(solution)/shard_map/exchange/pallas_call | solution.py:366
  283.2 8.7 %write_out.1 = (bf16[32,96,2048]{2,1,0:T(8,128)(2,1)}, bf16[32,96,2048]{2,1,0:T(8,128)(2,1)}, f32[32,96]{1,0:T(8,128)}, f32[32,96]{1,0:T(8,128)}, bf16[2048,128]{1,0:T(8,128)(2,1)}) custom-call(bf16[64,96,2048]{2,1,0:T(8,128)(2,1)S(1)} %get-tuple-element.13.pieces, bf16[8,4,32,256]{3,2,1,0:T(8,128)(2,1)S(1)} %get-tuple-element.14.routed, ...), custom_call_target="tpu_custom_call" | custom-call | tf_op jit(solution)/shard_map/write_out/pallas_call | solution.py:398

commit v4 on v3

--- a/solution.py
+++ b/solution.py
@@ -10,6 +10,7 @@
 MESH = pl.DeviceIdType.MESH
 WINDOW = 2
 LOADS = 3
+OPENING = 4
 LEAD = 4
 X_LAG, Y_LAG, HALF_LAG = 1, 2, 3
 HELD = LOADS + LEAD
@@ -36,7 +37,7 @@
     gate, up, router, gain,
     pieces, routed, scales,
     window, stage, weight, gains, part, early, partner, chip, others, whole,
-    load_sem, send_sem, recv_sem, pair_send, pair_recv, sum_send, sum_recv, last_send, last_recv,
+    load_sem, first_sem, send_sem, recv_sem, pair_send, pair_recv, sum_send, sum_recv, last_send, last_recv,
     early_send, early_recv, in_sem, r_send, r_recv, z_send, z_recv, c_send, c_recv,
 ):
     me, mine = lax.axis_index("rows"), lax.axis_index("owner")
@@ -207,9 +208,16 @@
         for i, p in enumerate(mates)
     ]
 
-    load(jnp.int32(0), True)
+    cut = gate.shape[1] // OPENING
+    opening = [
+        pltpu.make_async_copy(
+            gate.at[0, pl.ds(k * cut, cut)], window.at[0, pl.ds(k * cut, cut)], first_sem.at[k]
+        )
+        for k in range(OPENING)
+    ]
+    start(opening)
     start(fetch)
-    load(jnp.int32(0), False)
+    finish(opening)
     summed(jnp.int32(0))
     pl.semaphore_wait(barrier, len(peers) + jnp.where(mine > 0, 1, 0))
     start(direct(0)[::-1])
@@ -383,7 +391,7 @@
             pltpu.VMEM((units, 2, 1, half), jnp.float32),
             pltpu.VMEM((units, 2, 1, half), jnp.float32),
             pltpu.VMEM((units, 2, 1, half), jnp.float32),
-            dma((HELD,)), dma((WINDOW, n - 1)), dma((2 * WINDOW, n - 1)),
+            dma((HELD,)), dma((OPENING,)), dma((WINDOW, n - 1)), dma((2 * WINDOW, n - 1)),
             dma((SUMS,)), dma((SUMS,)), dma((SUMS, 2)), dma((SUMS, 2)), dma((SUMS,)), dma((SUMS,)),
             dma((2, n - 1)), dma((2, n - 1)), dma((2,)),
             dma((n // 2,)), dma((n // 2,)), dma((2, owners, n // 2)), dma((2, owners, n // 2)),

time: 292 us -> 292 us (level)
  no operation moved by 1% of the time
where the time goes in v4:
time: 292 us
  Pallas kernels  291 us (100%)
    pallas_call x1, Pallas kernels, in_kernels(): pl.pallas_call(functools.partial(exchange, experts, n, owners, float(dept...  283 us
    pallas_call x1, Pallas kernels, in_kernels(): pl.pallas_call(functools.partial(write_out, n), out_shape=(jax.ShapeDtype...  8.66 us

profile of v4, /device:TPU:1, one launch (start us, length us, event | category | flops | bytes accessed | tf_op | source)
XLA Modules:
  0.0 291.9 jit_solution(1650226317636391402)
XLA Ops:
  0.6 282.6 %exchange.1 = (bf16[64,96,2048]{2,1,0:T(8,128)(2,1)S(1)}, bf16[8,4,32,256]{3,2,1,0:T(8,128)(2,1)S(1)}, f32[64,1,768]{2,1,0:T(1,128)S(1)}) custom-call(f32[32,256,768]{2,1,0:T(8,128)} %gate.1, f32[32,256,768]{2,1,0:T(8,128)} %up.1, f32[32,256]{1,0:T(8,128)} %bitcast.4, f32[1,256]{1,0:T(1,128)} %bitcast.5), custom_call_target="tpu_custom_call" | custom-call | tf_op jit(solution)/shard_map/exchange/pallas_call | solution.py:374
  283.2 8.7 %write_out.1 = (bf16[32,96,2048]{2,1,0:T(8,128)(2,1)}, bf16[32,96,2048]{2,1,0:T(8,128)(2,1)}, f32[32,96]{1,0:T(8,128)}, f32[32,96]{1,0:T(8,128)}, bf16[2048,128]{1,0:T(8,128)(2,1)}) custom-call(bf16[64,96,2048]{2,1,0:T(8,128)(2,1)S(1)} %get-tuple-element.13.pieces, bf16[8,4,32,256]{3,2,1,0:T(8,128)(2,1)S(1)} %get-tuple-element.14.routed, ...), custom_call_target="tpu_custom_call" | custom-call | tf_op jit(solution)/shard_map/write_out/pallas_call | solution.py:406
